TPU v7x, 32 devices: a whole 2x2x4 slice. The times are simulated.
32 devices in a mesh: group: 2 (over x), tp: 4 (over z), dp: 4 (over y, core).
Axes of the slice: x: 2, y: 2, z: 4, core: 2. Of those that a mesh axis runs over, the one named last changes fastest.
Arguments:
- image_slots: bfloat16 [128, 8192], P(('group', 'tp'), 'dp'), may hold values from -6 to 6
- image_cot: bfloat16 [128, 8192], P(('group', 'tp'), 'dp'), may hold values from -6 to 6
- text_rows: bfloat16 [64, 8192], P(('group', 'tp'), 'dp'), may hold values from -6 to 6
- text_cot: bfloat16 [64, 8192], P(('group', 'tp'), 'dp'), may hold values from -6 to 6
- destination: int32 [64, 1], P(('group', 'tp')), may hold values from 0 to 1; in each aligned block of 8 rows (0 to 7, 8 to 15, ...) at most 8 rows name the same one
- text_count: int32 [8], P(('group', 'tp')), may hold values from 1 to 8, 48 in all
- w_gate: bfloat16 [8192, 14336], P('dp', 'tp'), may hold values from -0.0625 to 0.0625
- w_up: bfloat16 [8192, 14336], P('dp', 'tp'), may hold values from -0.0625 to 0.0625
- w_down: bfloat16 [14336, 8192], P('tp', 'dp'), may hold values from -0.046875 to 0.046875
Outputs:
- image_grad: bfloat16 [64, 8192], P(('group', 'tp'), 'dp')
- text_grad: bfloat16 [64, 8192], P(('group', 'tp'), 'dp')
Inputs may be any that keep to these rules, and one draw needn't show every extreme that they name: In the rows of one block of 8 rows no group is named more than 8 times, and some block names one group exactly 8 times; destination[i] decides which slot of image_slots and image_cot holds row i. Each block of 8 text rows has text_count live rows first; some block is full.
All inputs are finite; a program needn't handle non-finite values.
Results may differ from a plain program's by a relative error of at most 0.025.
Values may be sent and summed in bfloat16 or wider, within the bound.
No kernel may reach another device: no remote copies, remote signals or barrier semaphores. Data moves between devices by JAX's collectives and lax.ppermute only.
A program may use at most 128 MiB of HBM per device.

v0:
```python
import jax
import jax.numpy as jnp
from jax import lax
from jax.sharding import PartitionSpec as P


def language_grads(combined, w_gate, w_up, w_down):
    feat_dev = w_gate.shape[0]
    hidden_dev = w_gate.shape[1]
    piece = lax.all_gather(combined, "tp", axis=0, tiled=True)
    inputs_part = piece[:, :feat_dev]
    cot_part = piece[:, feat_dev:]
    gate = jnp.dot(inputs_part, w_gate, preferred_element_type=jnp.float32)
    up = jnp.dot(inputs_part, w_up, preferred_element_type=jnp.float32)
    back = lax.dot_general(
        cot_part, w_down, (((1,), (1,)), ((), ())), preferred_element_type=jnp.float32
    )
    partial_value = jnp.concatenate([gate, up, back], axis=1)
    sums = lax.psum_scatter(
        partial_value.astype(jnp.bfloat16), "dp", scatter_dimension=0, tiled=True
    ).astype(jnp.float32)
    gate = sums[:, :hidden_dev]
    up = sums[:, hidden_dev : 2 * hidden_dev]
    back = sums[:, 2 * hidden_dev :]
    sigmoid_gate = jax.nn.sigmoid(gate)
    dgate = (back * up * sigmoid_gate * (1.0 + gate * (1.0 - sigmoid_gate))).astype(jnp.bfloat16)
    dup = (back * gate * sigmoid_gate).astype(jnp.bfloat16)
    stacked = jnp.concatenate([dgate, dup], axis=1)
    piece = lax.all_gather(stacked, "dp", axis=0, tiled=True)
    total = lax.dot_general(
        piece[:, :hidden_dev], w_gate, (((1,), (1,)), ((), ())), preferred_element_type=jnp.float32
    )
    terms = total + lax.dot_general(
        piece[:, hidden_dev:], w_up, (((1,), (1,)), ((), ())), preferred_element_type=jnp.float32
    )
    return lax.psum_scatter(terms.astype(jnp.bfloat16), "tp", scatter_dimension=0, tiled=True)


def per_device(
    image_slots, image_cot, text_rows, text_cot, destination, text_count, w_gate, w_up, w_down
):
    groups = lax.axis_size("group")
    slot_dev = image_slots.shape[0]
    capacity = slot_dev // groups
    image_dev = destination.shape[0]
    text_dev = text_rows.shape[0]
    target = destination[:, 0]
    position = lax.broadcasted_iota(jnp.int32, (image_dev, image_dev), 0)
    other = lax.broadcasted_iota(jnp.int32, (image_dev, image_dev), 1)
    same = (target[:, None] == target[None, :]) & (other < position)
    rank = jnp.sum(same.astype(jnp.int32), axis=1)
    column = target * capacity + rank
    slot_index = lax.broadcasted_iota(jnp.int32, (image_dev, slot_dev), 1)
    select = (column[:, None] == slot_index).astype(jnp.bfloat16)
    text_both = jnp.concatenate([text_rows, text_cot], axis=1)
    both = jnp.concatenate([image_slots, image_cot], axis=1)
    arrived = lax.all_to_all(both, "group", split_axis=0, concat_axis=0, tiled=True)
    picked = jnp.dot(select, arrived, preferred_element_type=jnp.float32).astype(jnp.bfloat16)
    combined = jnp.concatenate([picked, text_both], axis=0)
    grads = language_grads(combined, w_gate, w_up, w_down)
    image_grad = grads[:image_dev]
    text_part = grads[image_dev:]
    live = lax.broadcasted_iota(jnp.int32, (text_dev, 1), 0) < text_count[0]
    text_grad = jnp.where(live, text_part, jnp.zeros_like(text_part))
    return (image_grad, text_grad)


def solution(mesh):
    placed = (
        P(("group", "tp"), "dp"),
        P(("group", "tp"), "dp"),
        P(("group", "tp"), "dp"),
        P(("group", "tp"), "dp"),
        P(("group", "tp"), None),
        P(("group", "tp")),
        P("dp", "tp"),
        P("dp", "tp"),
        P("tp", "dp"),
    )
    return jax.shard_map(
        per_device,
        mesh=mesh,
        in_specs=placed,
        out_specs=(P(("group", "tp"), "dp"), P(("group", "tp"), "dp")),
        check_vma=False,
    )
```

profile of v0, /device:TPU:0, one launch (start us, length us, event | category | flops | bytes accessed | tf_op | source)
XLA Modules:
  0.0 142.4 jit_solution(585150537257338750)
XLA Ops:
  7.2 1.5 %maximum_bitcast_fusion = bf16[2,8,4096]{2,1,0:T(8,128)(2,1)} fusion(bf16[16,2048]{1,0:T(8,128)(2,1)} %param.10, bf16[16,2048]{1,0:T(8,128)(2,1)} %param.9), kind=kLoop, calls=%fused_computation.20 | loop fusion | flops 262144 | bytes 262144 | tf_op jit(solution)/shard_map/all_to_all | solution.py:57
  8.7 4.2 %all-to-all-start = ((bf16[2,8,4096]{2,1,0:T(8,128)(2,1)}), bf16[2,8,4096]{2,1,0:T(8,128)(2,1)S(1)}, u32[]{:S(2)}, u32[]{:S(2)}) async-start(bf16[2,8,4096]{2,1,0:T(8,128)(2,1)} %maximum_bitcast_fusion), calls=%async_computation | async-start | bytes 262144 | tf_op jit(solution)/shard_map/all_to_all | solution.py:57
  12.9 0.0 reduce-scatter.3.cloned.1.call-start
  12.9 0.9 convert_reduce_fusion
  13.8 0.7 fusion.13
  14.5 3.0 %all-to-all-done = bf16[2,8,4096]{2,1,0:T(8,128)(2,1)S(1)} async-done(((bf16[2,8,4096]{2,1,0:T(8,128)(2,1)}), bf16[2,8,4096]{2,1,0:T(8,128)(2,1)S(1)}, u32[]{:S(2)}, u32[]{:S(2)}) %all-to-all-start) | async-done | bytes 131104 | tf_op jit(solution)/shard_map/all_to_all | solution.py:57
  17.5 0.2 convolution_convert_fusion.3
  17.7 0.8 maximum_maximum_fusion
  18.5 15.6 %all_gather.6 = bf16[64,4096]{1,0:T(8,128)(2,1)S(1)} all-gather(bf16[16,4096]{1,0:T(8,128)(2,1)S(1)} %maximum_maximum_fusion), channel_id=1, replica_groups=mesh['group'=2,'tp'=4,'dp'=4] {'tp'}, dimensions={0}, use_global_device_ids=true | all-gather | bytes 655360 | tf_op jit(solution)/shard_map/all_gather | solution.py:10
  34.1 0.0 slice-start
  34.1 0.0 slice-start.1
  34.1 9.9 %convolution_convert_fusion = bf16[64,3584]{1,0:T(8,128)(2,1)S(1)} fusion(bf16[3584,2048]{1,0:T(8,128)(2,1)} %param.17, bf16[64,4096]{1,0:T(8,128)(2,1)S(1)} %all_gather.6), kind=kOutput, calls=%fused_computation | convolution fusion | flops 939753472 | bytes 15400960 | tf_op jit(solution)/shard_map/dot_general | solution.py:15
  43.9 0.0 slice-start.2
  43.9 0.0 slice-start.3
  44.0 8.0 %convolution_convert_fusion.1 = bf16[64,3584]{1,0:T(8,128)(2,1)S(1)} fusion(bf16[2048,3584]{1,0:T(8,128)(2,1)} %param.16, bf16[64,4096]{1,0:T(8,128)(2,1)S(1)} %all_gather.6), kind=kOutput, calls=%fused_computation.1 | convolution fusion | flops 939753472 | bytes 15400960 | tf_op jit(solution)/shard_map/dot_general | solution.py:14
  51.9 0.0 slice-done
  51.9 0.0 slice-done.1
  51.9 0.0 slice-done.2
  51.9 0.0 slice-done.3
  52.0 2.6 %convolution_convert_fusion.2 = bf16[64,3584]{1,0:T(8,128)(2,1)S(1)} fusion(bf16[2048,3584]{1,0:T(8,128)(2,1)S(1)} %bitcast.20, bf16[64,4096]{1,0:T(8,128)(2,1)S(1)} %all_gather.6), kind=kOutput, calls=%fused_computation.2 | convolution fusion | flops 939753472 | bytes 15400960 | tf_op jit(solution)/shard_map/dot_general | solution.py:13
  54.6 1.2 pad_maximum_fusion
  55.8 0.0 reduce-scatter.3.cloned.1.call-update
  55.8 0.0 reduce-scatter.5.cloned.1.call-start
  55.9 27.5 %reduce-scatter.3.cloned.1.call-done = bf16[16,10752]{1,0:T(8,128)(2,1)} async-done(((bf16[64,10752]{1,0:T(8,128)(2,1)}), bf16[16,10752]{1,0:T(8,128)(2,1)}) %reduce-scatter.3.cloned.1.call-update) | async-done | bytes 344080 | tf_op jit(solution)/shard_map/reduce_scatter | solution.py:19
  83.4 1.0 convert_element_type.22
  84.4 0.1 fusion.9
  84.6 8.7 %all_gather.7 = bf16[64,7168]{1,0:T(8,128)(2,1)S(1)} all-gather(bf16[16,7168]{1,0:T(8,128)(2,1)S(1)} %pad_maximum_fusion.1), channel_id=1, replica_groups=mesh['group'=2,'tp'=4,'dp'=4] {'dp'}, dimensions={0}, use_global_device_ids=true | all-gather | bytes 1146880 | tf_op jit(solution)/shard_map/all_gather | solution.py:29
  93.3 9.7 %fusion.2 = f32[64,2048]{1,0:T(8,128)S(1)} fusion(bf16[2048,3584]{1,0:T(8,128)(2,1)} %param.15, bf16[64,7168]{1,0:T(8,128)(2,1)S(1)} %all_gather.7), kind=kOutput, calls=%fused_computation.8 | convolution fusion | flops 939524096 | bytes 15663104 | tf_op jit(solution)/shard_map/dot_general | solution.py:30
  102.9 10.4 %fusion = bf16[64,2048]{1,0:T(8,128)(2,1)} fusion(f32[64,2048]{1,0:T(8,128)S(1)} %fusion.2, bf16[2048,3584]{1,0:T(8,128)(2,1)} %param.16, bf16[64,7168]{1,0:T(8,128)(2,1)S(1)} %all_gather.7), kind=kOutput, calls=%fused_computation.5 | convolution fusion | flops 939786240 | bytes 15925248 | tf_op jit(solution)/shard_map/dot_general | solution.py:33
  113.3 0.0 reduce-scatter.5.cloned.1.call-update
  114.0 20.1 %reduce-scatter.5.cloned.1.call-done = bf16[16,2048]{1,0:T(8,128)(2,1)} async-done(((bf16[64,2048]{1,0:T(8,128)(2,1)}), bf16[16,2048]{1,0:T(8,128)(2,1)}) %reduce-scatter.5.cloned.1.call-update) | async-done | bytes 65552 | tf_op jit(solution)/shard_map/reduce_scatter | solution.py:36
  134.1 1.5 %slice_select_fusion = (bf16[8,2048]{1,0:T(8,128)(2,1)}, bf16[8,2048]{1,0:T(8,128)(2,1)}) fusion(bf16[16,2048]{1,0:T(8,128)(2,1)} %reduce-scatter.5.cloned.1.call-done, pred[8]{0:T(512)(128)(4,1)S(1)} %iota_compare_fusion.3), kind=kLoop, calls=%fused_computation.23 | loop fusion | flops 16384 | bytes 131080 | tf_op jit(solution)/shard_map/jit(_where)/select_n | solution.py:64
  (3 shorter events, 0.0 us)
Async XLA Ops:
  8.7 8.8 %all-to-all-start = ((bf16[2,8,4096]{2,1,0:T(8,128)(2,1)}), bf16[2,8,4096]{2,1,0:T(8,128)(2,1)S(1)}, u32[]{:S(2)}, u32[]{:S(2)}) async-start(bf16[2,8,4096]{2,1,0:T(8,128)(2,1)} %maximum_bitcast_fusion), calls=%async_computation | async-start | bytes 262144 | tf_op jit(solution)/shard_map/all_to_all | solution.py:57
  12.9 70.5 %reduce-scatter.3.cloned.1.call-start = ((), (), s32[]{:S(2)}) async-start(), calls=%async_computation.3 | async-start | bytes 1720320 | tf_op jit(solution)/shard_map/reduce_scatter | solution.py:19
  34.1 17.8 %slice-start = ((s8[14680064]{0:T(1024)(128)(4,1)}), s8[4194304]{0:T(1024)(128)(4,1)S(1)}, s32[]{:S(2)}) async-start(s8[14680064]{0:T(1024)(128)(4,1)} %bitcast.19), calls=%async_computation.5 | async-start | bytes 8388608
  34.1 17.9 %slice-start.1 = ((s8[14680064]{0:T(1024)(128)(4,1)}), s8[2097152]{0:T(1024)(128)(4,1)S(1)}, s32[]{:S(2)}) async-start(s8[14680064]{0:T(1024)(128)(4,1)} %bitcast.19), calls=%async_computation.6 | async-start | bytes 4194304
  43.9 8.0 %slice-start.2 = ((s8[14680064]{0:T(1024)(128)(4,1)}), s8[4194304]{0:T(1024)(128)(4,1)S(1)}, s32[]{:S(2)}) async-start(s8[14680064]{0:T(1024)(128)(4,1)} %bitcast.19), calls=%async_computation.7 | async-start | bytes 8388608
  43.9 8.0 %slice-start.3 = ((s8[14680064]{0:T(1024)(128)(4,1)}), s8[4194304]{0:T(1024)(128)(4,1)S(1)}, s32[]{:S(2)}) async-start(s8[14680064]{0:T(1024)(128)(4,1)} %bitcast.19), calls=%async_computation.8 | async-start | bytes 8388608
  55.8 78.3 %reduce-scatter.5.cloned.1.call-start = ((), (), s32[]{:S(2)}) async-start(), calls=%async_computation.4 | async-start | bytes 327680 | tf_op jit(solution)/shard_map/reduce_scatter | solution.py:36
Sparse Core Ops, SparseCore 0:
  55.9 27.4 reduce-scatter.2
  113.5 20.5 reduce-scatter.4
where the time goes:
time: 143 us; the launch traced here: 142 us
  waiting for transfers between devices  50.6 us (35%)
  matrix products  40.7 us (28%)
  blocking collectives  24.3 us (17%)
  between operations  14.8 us (10%)
  other arithmetic  7.71 us (5%)
  starting transfers between devices  4.28 us (3%)
    reduce_scatter x1, waiting for transfers between devices, language_grads(): lax.psum_scatter(partial_value.astype(jnp.bfloat16), 'dp', scatter_dimens...  27.5 us
    reduce_scatter x1, waiting for transfers between devices, language_grads(): lax.psum_scatter(terms.astype(jnp.bfloat16), 'tp', scatter_dimension=0, t...  20.1 us
    all_gather x1, blocking collectives, language_grads(): piece = lax.all_gather(combined, 'tp', axis=0, tiled=True)  15.6 us
    dot_general x1, matrix products, language_grads(): lax.dot_general(piece[:, hidden_dev:], w_up, (((1,), (1,)), ((), ())), pr...  10.4 us
    dot_general x1, matrix products, language_grads(): lax.dot_general(cot_part, w_down, (((1,), (1,)), ((), ())), preferred_ele...  9.86 us
    dot_general x1, matrix products, language_grads(): lax.dot_general(piece[:, :hidden_dev], w_gate, (((1,), (1,)), ((), ())),...  9.67 us
    all_gather x1, blocking collectives, language_grads(): piece = lax.all_gather(stacked, 'dp', axis=0, tiled=True)  8.72 us
    dot_general x1, matrix products, language_grads(): up = jnp.dot(inputs_part, w_up, preferred_element_type=jnp.float32)  7.95 us
  transfers between devices with their start and end apart: 3, of which 3 were waited for; matrix products, arithmetic and copies ran while one was open for 1% of the time, Pallas kernels for 0%

commit v1 on v0

--- a/solution.py
+++ b/solution.py
@@ -26,7 +26,12 @@
     dgate = (back * up * sigmoid_gate * (1.0 + gate * (1.0 - sigmoid_gate))).astype(jnp.bfloat16)
     dup = (back * gate * sigmoid_gate).astype(jnp.bfloat16)
     stacked = jnp.concatenate([dgate, dup], axis=1)
-    piece = lax.all_gather(stacked, "dp", axis=0, tiled=True)
+    ring = [stacked]
+    for hop in range(3):
+        ring.append(lax.ppermute(ring[-1], "dp", [(dev, (dev + 1) % 4) for dev in range(4)]))
+    piece = jnp.roll(
+        jnp.concatenate(ring[::-1], axis=0), (lax.axis_index("dp") + 1) * ring[0].shape[0], axis=0
+    )
     total = lax.dot_general(
         piece[:, :hidden_dev], w_gate, (((1,), (1,)), ((), ())), preferred_element_type=jnp.float32
     )

time: 143 us -> 150 us (1.049)
  waiting for transfers between devices: 50.6 us -> 66.4 us
  blocking collectives: 24.3 us -> 15.6 us
    ppermute x0 -> x3, waiting for transfers between devices: none -> 16.3 us  [language_grads(): lax.ppermute(ring[-1], 'dp', [(dev, (dev + 1) % 4) for dev in range(4)])]
    all_gather x1 -> x0, blocking collectives: 8.72 us -> none  [language_grads(): piece = lax.all_gather(stacked, 'dp', axis=0, tiled=True)]
  transfers between devices with their start and end apart: 3 -> 6, of which waited for: 3 -> 6; matrix products, arithmetic and copies ran while one was open for 1% -> 1% of each run, Pallas kernels for 0% -> 0%
where the time goes in v1:
time: 150 us
  waiting for transfers between devices  66.4 us (44%)
  matrix products  40.7 us (27%)
  blocking collectives  15.6 us (10%)
  between operations  14.8 us (10%)
  other arithmetic  7.75 us (5%)
  starting transfers between devices  4.34 us (3%)
    reduce_scatter x1, waiting for transfers between devices, language_grads(): lax.psum_scatter(partial_value.astype(jnp.bfloat16), 'dp', scatter_dimens...  27.5 us
    reduce_scatter x1, waiting for transfers between devices, language_grads(): lax.psum_scatter(terms.astype(jnp.bfloat16), 'tp', scatter_dimension=0, t...  19.5 us
    ppermute x3, waiting for transfers between devices, language_grads(): lax.ppermute(ring[-1], 'dp', [(dev, (dev + 1) % 4) for dev in range(4)])  16.3 us
    all_gather x1, blocking collectives, language_grads(): piece = lax.all_gather(combined, 'tp', axis=0, tiled=True)  15.6 us
    dot_general x1, matrix products, language_grads(): lax.dot_general(piece[:, :hidden_dev], w_gate, (((1,), (1,)), ((), ())),...  10.4 us
    dot_general x1, matrix products, language_grads(): lax.dot_general(cot_part, w_down, (((1,), (1,)), ((), ())), preferred_ele...  9.86 us
    dot_general x1, matrix products, language_grads(): lax.dot_general(piece[:, hidden_dev:], w_up, (((1,), (1,)), ((), ())), pr...  9.67 us
    dot_general x1, matrix products, language_grads(): up = jnp.dot(inputs_part, w_up, preferred_element_type=jnp.float32)  7.96 us
  transfers between devices with their start and end apart: 6, of which 6 were waited for; matrix products, arithmetic and copies ran while one was open for 1% of the time, Pallas kernels for 0%

profile of v1, /device:TPU:0, one launch (start us, length us, event | category | flops | bytes accessed | tf_op | source)
XLA Modules:
  0.0 149.7 jit_solution(3277791591593666196)
XLA Ops:
  7.2 1.5 %maximum_bitcast_fusion = bf16[2,8,4096]{2,1,0:T(8,128)(2,1)} fusion(bf16[16,2048]{1,0:T(8,128)(2,1)} %param.10, bf16[16,2048]{1,0:T(8,128)(2,1)} %param.9), kind=kLoop, calls=%fused_computation.20 | loop fusion | flops 262144 | bytes 262144 | tf_op jit(solution)/shard_map/all_to_all | solution.py:62
  8.7 4.2 %all-to-all-start = ((bf16[2,8,4096]{2,1,0:T(8,128)(2,1)}), bf16[2,8,4096]{2,1,0:T(8,128)(2,1)S(1)}, u32[]{:S(2)}, u32[]{:S(2)}) async-start(bf16[2,8,4096]{2,1,0:T(8,128)(2,1)} %maximum_bitcast_fusion), calls=%async_computation | async-start | bytes 262144 | tf_op jit(solution)/shard_map/all_to_all | solution.py:62
  12.9 0.0 reduce-scatter.3.cloned.1.call-start
  12.9 0.9 convert_reduce_fusion
  13.8 0.7 fusion.13
  14.5 3.0 %all-to-all-done = bf16[2,8,4096]{2,1,0:T(8,128)(2,1)S(1)} async-done(((bf16[2,8,4096]{2,1,0:T(8,128)(2,1)}), bf16[2,8,4096]{2,1,0:T(8,128)(2,1)S(1)}, u32[]{:S(2)}, u32[]{:S(2)}) %all-to-all-start) | async-done | bytes 131104 | tf_op jit(solution)/shard_map/all_to_all | solution.py:62
  17.5 0.2 convolution_convert_fusion.3
  17.7 0.8 maximum_maximum_fusion
  18.5 15.6 %all_gather.3 = bf16[64,4096]{1,0:T(8,128)(2,1)S(1)} all-gather(bf16[16,4096]{1,0:T(8,128)(2,1)S(1)} %maximum_maximum_fusion), channel_id=1, replica_groups=mesh['group'=2,'tp'=4,'dp'=4] {'tp'}, dimensions={0}, use_global_device_ids=true | all-gather | bytes 655360 | tf_op jit(solution)/shard_map/all_gather | solution.py:10
  34.1 9.9 %convolution_convert_fusion = bf16[64,3584]{1,0:T(8,128)(2,1)S(1)} fusion(bf16[3584,2048]{1,0:T(8,128)(2,1)} %param.17, bf16[64,4096]{1,0:T(8,128)(2,1)S(1)} %all_gather.3), kind=kOutput, calls=%fused_computation | convolution fusion | flops 939753472 | bytes 15400960 | tf_op jit(solution)/shard_map/dot_general | solution.py:15
  43.9 0.0 slice-start.2
  44.0 0.0 slice-start.3
  44.0 8.0 %convolution_convert_fusion.1 = bf16[64,3584]{1,0:T(8,128)(2,1)S(1)} fusion(bf16[2048,3584]{1,0:T(8,128)(2,1)} %param.16, bf16[64,4096]{1,0:T(8,128)(2,1)S(1)} %all_gather.3), kind=kOutput, calls=%fused_computation.1 | convolution fusion | flops 939753472 | bytes 15400960 | tf_op jit(solution)/shard_map/dot_general | solution.py:14
  51.9 0.0 slice-done
  52.0 2.6 %convolution_convert_fusion.2 = bf16[64,3584]{1,0:T(8,128)(2,1)S(1)} fusion(bf16[2048,3584]{1,0:T(8,128)(2,1)S(1)} %bitcast.20, bf16[64,4096]{1,0:T(8,128)(2,1)S(1)} %all_gather.3), kind=kOutput, calls=%fused_computation.2 | convolution fusion | flops 939753472 | bytes 15400960 | tf_op jit(solution)/shard_map/dot_general | solution.py:13
  54.6 1.2 pad_maximum_fusion
  55.8 0.0 reduce-scatter.3.cloned.1.call-update
  55.8 0.0 reduce-scatter.5.cloned.1.call-start
  55.9 27.5 %reduce-scatter.3.cloned.1.call-done = bf16[16,10752]{1,0:T(8,128)(2,1)} async-done(((bf16[64,10752]{1,0:T(8,128)(2,1)}), bf16[16,10752]{1,0:T(8,128)(2,1)}) %reduce-scatter.3.cloned.1.call-update) | async-done | bytes 344080 | tf_op jit(solution)/shard_map/reduce_scatter | solution.py:19
  83.4 1.0 convert_element_type.22
  84.4 0.1 fusion.9
  84.6 0.1 collective-permute-start
  84.6 5.4 %collective-permute-done = bf16[16,7168]{1,0:T(8,128)(2,1)S(1)} collective-permute-done((bf16[16,7168]{1,0:T(8,128)(2,1)S(1)}, bf16[16,7168]{1,0:T(8,128)(2,1)S(1)}, u32[]{:S(2)}, u32[]{:S(2)}) %collective-permute-start) | collective-permute-done | bytes 229408 | tf_op jit(solution)/shard_map/ppermute | solution.py:31
  90.1 0.0 collective-permute-start.1
  90.1 5.4 %collective-permute-done.1 = bf16[16,7168]{1,0:T(8,128)(2,1)S(1)} collective-permute-done((bf16[16,7168]{1,0:T(8,128)(2,1)S(1)}, bf16[16,7168]{1,0:T(8,128)(2,1)S(1)}, u32[]{:S(2)}, u32[]{:S(2)}) %collective-permute-start.1) | collective-permute-done | bytes 229408 | tf_op jit(solution)/shard_map/ppermute | solution.py:31
  95.5 0.0 collective-permute-start.2
  95.5 5.4 %collective-permute-done.2 = bf16[16,7168]{1,0:T(8,128)(2,1)S(1)} collective-permute-done((bf16[16,7168]{1,0:T(8,128)(2,1)S(1)}, bf16[16,7168]{1,0:T(8,128)(2,1)S(1)}, u32[]{:S(2)}, u32[]{:S(2)}) %collective-permute-start.2) | collective-permute-done | bytes 229408 | tf_op jit(solution)/shard_map/ppermute | solution.py:31
  101.2 9.7 %fusion.1 = f32[64,2048]{1,0:T(8,128)S(1)} fusion(bf16[2048,3584]{1,0:T(8,128)(2,1)} %param.16, bf16[128,7168]{1,0:T(8,128)(2,1)S(1)} %constant_dynamic-update-slice_fusion, s32[]{:T(128)S(6)} %select_n.18, s32[]{:T(128)S(6)} %add.37), kind=kOutput, calls=%fused_computation.7 | convolution fusion | flops 939524096 | bytes 15663112 | tf_op jit(solution)/shard_map/dot_general | solution.py:38
  110.8 10.4 %fusion = bf16[64,2048]{1,0:T(8,128)(2,1)} fusion(f32[64,2048]{1,0:T(8,128)S(1)} %fusion.1, bf16[2048,3584]{1,0:T(8,128)(2,1)} %param.15, bf16[128,7168]{1,0:T(8,128)(2,1)S(1)} %constant_dynamic-update-slice_fusion, s32[]{:T(128)S(6)} %select_n.18), kind=kOutput, calls=%fused_computation.5 | convolution fusion | flops 939786240 | bytes 15925252 | tf_op jit(solution)/shard_map/dot_general | solution.py:35
  121.2 0.0 reduce-scatter.5.cloned.1.call-update
  121.9 19.5 %reduce-scatter.5.cloned.1.call-done = bf16[16,2048]{1,0:T(8,128)(2,1)} async-done(((bf16[64,2048]{1,0:T(8,128)(2,1)}), bf16[16,2048]{1,0:T(8,128)(2,1)}) %reduce-scatter.5.cloned.1.call-update) | async-done | bytes 65552 | tf_op jit(solution)/shard_map/reduce_scatter | solution.py:41
  141.4 1.5 slice_select_fusion
  (16 shorter events, 0.2 us)
Async XLA Ops:
  8.7 8.8 %all-to-all-start = ((bf16[2,8,4096]{2,1,0:T(8,128)(2,1)}), bf16[2,8,4096]{2,1,0:T(8,128)(2,1)S(1)}, u32[]{:S(2)}, u32[]{:S(2)}) async-start(bf16[2,8,4096]{2,1,0:T(8,128)(2,1)} %maximum_bitcast_fusion), calls=%async_computation | async-start | bytes 262144 | tf_op jit(solution)/shard_map/all_to_all | solution.py:62
  12.9 70.5 %reduce-scatter.3.cloned.1.call-start = ((), (), s32[]{:S(2)}) async-start(), calls=%async_computation.3 | async-start | bytes 1720320 | tf_op jit(solution)/shard_map/reduce_scatter | solution.py:19
  34.1 17.8 %slice-start = ((s8[14680064]{0:T(1024)(128)(4,1)}), s8[4194304]{0:T(1024)(128)(4,1)S(1)}, s32[]{:S(2)}) async-start(s8[14680064]{0:T(1024)(128)(4,1)} %bitcast.19), calls=%async_computation.5 | async-start | bytes 8388608
  34.1 17.9 %slice-start.1 = ((s8[14680064]{0:T(1024)(128)(4,1)}), s8[2097152]{0:T(1024)(128)(4,1)S(1)}, s32[]{:S(2)}) async-start(s8[14680064]{0:T(1024)(128)(4,1)} %bitcast.19), calls=%async_computation.6 | async-start | bytes 4194304
  43.9 8.0 %slice-start.2 = ((s8[14680064]{0:T(1024)(128)(4,1)}), s8[4194304]{0:T(1024)(128)(4,1)S(1)}, s32[]{:S(2)}) async-start(s8[14680064]{0:T(1024)(128)(4,1)} %bitcast.19), calls=%async_computation.7 | async-start | bytes 8388608
  44.0 8.0 %slice-start.3 = ((s8[14680064]{0:T(1024)(128)(4,1)}), s8[4194304]{0:T(1024)(128)(4,1)S(1)}, s32[]{:S(2)}) async-start(s8[14680064]{0:T(1024)(128)(4,1)} %bitcast.19), calls=%async_computation.8 | async-start | bytes 8388608
  55.8 85.6 %reduce-scatter.5.cloned.1.call-start = ((), (), s32[]{:S(2)}) async-start(), calls=%async_computation.4 | async-start | bytes 327680 | tf_op jit(solution)/shard_map/reduce_scatter | solution.py:41
  84.6 5.5 %collective-permute-start = (bf16[16,7168]{1,0:T(8,128)(2,1)S(1)}, bf16[16,7168]{1,0:T(8,128)(2,1)S(1)}, u32[]{:S(2)}, u32[]{:S(2)}) collective-permute-start(bf16[16,7168]{1,0:T(8,128)(2,1)S(1)} %pad_maximum_fusion.1), channel_id=1, source_target_pairs={{0,1},{1,2},{2,3},{3,0},{4,5},{5,6},{6,7},{7,4},{8,9},{9,10},{10,1... | collective-permute-start | bytes 688136 | tf_op jit(solution)/shard_map/ppermute | solution.py:31
  90.1 5.4 %collective-permute-start.1 = (bf16[16,7168]{1,0:T(8,128)(2,1)S(1)}, bf16[16,7168]{1,0:T(8,128)(2,1)S(1)}, u32[]{:S(2)}, u32[]{:S(2)}) collective-permute-start(bf16[16,7168]{1,0:T(8,128)(2,1)S(1)} %collective-permute-done), channel_id=1, source_target_pairs={{0,1},{1,2},{2,3},{3,0},{4,5},{5,6},{6,7},{7,4},{8,9},{9,10},{10,1... | collective-permute-start | bytes 688136 | tf_op jit(solution)/shard_map/ppermute | solution.py:31
  95.5 5.4 %collective-permute-start.2 = (bf16[16,7168]{1,0:T(8,128)(2,1)S(1)}, bf16[16,7168]{1,0:T(8,128)(2,1)S(1)}, u32[]{:S(2)}, u32[]{:S(2)}) collective-permute-start(bf16[16,7168]{1,0:T(8,128)(2,1)S(1)} %collective-permute-done.1), channel_id=1, source_target_pairs={{0,1},{1,2},{2,3},{3,0},{4,5},{5,6},{6,7},{7,4},{8,9},{9,10},{10,1... | collective-permute-start | bytes 688136 | tf_op jit(solution)/shard_map/ppermute | solution.py:31
Sparse Core Ops, SparseCore 0:
  55.9 27.4 reduce-scatter.2
  121.4 19.9 reduce-scatter.4
